TPU v7x, 32 devices: a whole 2x2x4 slice. The times are simulated.
32 devices in a mesh: dp: 2 (over x), fsdp: 16 (over z, y, core).
Axes of the slice: x: 2, y: 2, z: 4, core: 2. Of those that a mesh axis runs over, the one named last changes fastest.
Arguments:
- inputs: bfloat16 [32, 512, 768], P(('dp', 'fsdp')), may hold values from -6 to 6
- segments: int32 [32, 512], P(('dp', 'fsdp')), may hold values from 0 to 3, never falling along the last dimension, each value on 1 to 256 neighbouring positions
- out_grads: bfloat16 [4, 32, 512, 768], P(None, ('dp', 'fsdp')), may hold values from -6 to 6
- query_weight: bfloat16 [768, 768], P(('dp', 'fsdp')), may hold values from -0.21875 to 0.21875
- query_bias: bfloat16 [768], P(('dp', 'fsdp')), may hold values from -1.1953125 to 1.1953125
- key_weight: bfloat16 [768, 768], P(('dp', 'fsdp')), may hold values from -0.21875 to 0.21875
- value_weight: bfloat16 [768, 768], P(('dp', 'fsdp')), may hold values from -0.21875 to 0.21875
- value_bias: bfloat16 [768], P(('dp', 'fsdp')), may hold values from -1.1953125 to 1.1953125
- output_weight: bfloat16 [768, 768], P(('dp', 'fsdp')), may hold values from -2.5 to 2.5
- output_bias: bfloat16 [768], P(('dp', 'fsdp')), may hold values from -1.1953125 to 1.1953125
- first_gain: bfloat16 [768], P(('dp', 'fsdp')), may hold values from 0.5 to 1.5
- first_shift: bfloat16 [768], P(('dp', 'fsdp')), may hold values from -1.1953125 to 1.1953125
- inner_weight: bfloat16 [768, 3072], P(('dp', 'fsdp')), may hold values from -0.21875 to 0.21875
- inner_bias: bfloat16 [3072], P(('dp', 'fsdp')), may hold values from -1.1953125 to 1.1953125
- outer_weight: bfloat16 [3072, 768], P(('dp', 'fsdp')), may hold values from -0.21875 to 0.21875
- outer_bias: bfloat16 [768], P(('dp', 'fsdp')), may hold values from -1.1953125 to 1.1953125
- second_gain: bfloat16 [768], P(('dp', 'fsdp')), may hold values from 0.5 to 1.5
- second_shift: bfloat16 [768], P(('dp', 'fsdp')), may hold values from -1.1953125 to 1.1953125
Outputs:
- outputs: bfloat16 [4, 32, 512, 768], P(None, ('dp', 'fsdp'))
- input_grad: float32 [32, 512, 768], P(('dp', 'fsdp'))
- query_weight_grad: float32 [768, 768], P(('dp', 'fsdp'))
- query_bias_grad: float32 [768], P(('dp', 'fsdp'))
- key_weight_grad: float32 [768, 768], P(('dp', 'fsdp'))
- value_weight_grad: float32 [768, 768], P(('dp', 'fsdp'))
- value_bias_grad: float32 [768], P(('dp', 'fsdp'))
- output_weight_grad: float32 [768, 768], P(('dp', 'fsdp'))
- output_bias_grad: float32 [768], P(('dp', 'fsdp'))
- first_gain_grad: float32 [768], P(('dp', 'fsdp'))
- first_shift_grad: float32 [768], P(('dp', 'fsdp'))
- inner_weight_grad: float32 [768, 3072], P(('dp', 'fsdp'))
- inner_bias_grad: float32 [3072], P(('dp', 'fsdp'))
- outer_weight_grad: float32 [3072, 768], P(('dp', 'fsdp'))
- outer_bias_grad: float32 [768], P(('dp', 'fsdp'))
- second_gain_grad: float32 [768], P(('dp', 'fsdp'))
- second_shift_grad: float32 [768], P(('dp', 'fsdp'))
Inputs may be any that keep to these rules, and one draw needn't show every extreme that they name: `segments`: in each row the segment numbers start at 0, never fall, and each of the 4 examples holds 1 to 256 tokens.
All inputs are finite; a program needn't handle non-finite values.
Results may differ from a plain program's by a relative error of at most 0.014.
Values may be sent and summed in bfloat16 or wider, within the bound.
A program may use at most 256 MiB of HBM per device.

v0:
```python
import jax
import jax.numpy as jnp
from jax import lax
from jax.sharding import PartitionSpec as P

HEADS = 12
DH = 64
FF = 3072
WIDTHS = 4


EPSILON = 1e-12
SCORE_SCALE = 0.125
MASKED = -1000000000.0


def matmul(left, right):
    return jnp.dot(left, right, preferred_element_type=jnp.float32)


def matmul_tn(left, right):
    return lax.dot_general(
        left, right, (((0,), (0,)), ((), ())), preferred_element_type=jnp.float32
    )


def matmul_nt(left, right):
    return lax.dot_general(
        left, right, (((1,), (1,)), ((), ())), preferred_element_type=jnp.float32
    )


def normalize(hidden, gain, shift):
    center = hidden - jnp.mean(hidden, axis=-1, keepdims=True)
    inverse = lax.rsqrt(jnp.mean(center * center, axis=-1, keepdims=True) + EPSILON)
    scaled = center * inverse
    return (scaled * gain + shift, scaled, inverse)


def norm_back(upstream, scaled, inverse, gain):
    times_gain = upstream * gain
    centered = times_gain - jnp.mean(times_gain, axis=-1, keepdims=True)
    return (centered - scaled * jnp.mean(times_gain * scaled, axis=-1, keepdims=True)) * inverse


def split_heads(values, head_count):
    return values.reshape(values.shape[0], head_count, DH).transpose(1, 0, 2)


def merge_heads(stacked):
    return stacked.transpose(1, 0, 2).reshape(stacked.shape[1], stacked.shape[0] * stacked.shape[2])


def head_forward(packed, same_seg):
    query_rows, key_rows, value_rows = packed
    scores = jnp.where(same_seg, matmul_nt(query_rows, key_rows) * SCORE_SCALE, MASKED)
    row_max = jnp.max(scores, axis=-1, keepdims=True)
    exp_scores = jnp.exp(scores - row_max)
    row_total = jnp.sum(exp_scores, axis=-1, keepdims=True)
    attn_probs = (exp_scores / row_total).astype(jnp.bfloat16)
    return (matmul(attn_probs, value_rows), (row_max + jnp.log(row_total))[:, 0])


def head_backward(packed, same_seg):
    query_rows, key_rows, value_rows, grad_rows, log_total = packed
    scores = jnp.where(same_seg, matmul_nt(query_rows, key_rows) * SCORE_SCALE, MASKED)
    attn_probs = jnp.exp(scores - log_total[:, None])
    value_grad = matmul_tn(attn_probs.astype(jnp.bfloat16), grad_rows)
    prob_grad = matmul_nt(grad_rows, value_rows)
    score_grad = (
        attn_probs * (prob_grad - jnp.sum(prob_grad * attn_probs, axis=-1, keepdims=True))
    ).astype(jnp.bfloat16)
    query_grad = matmul(score_grad, key_rows) * SCORE_SCALE
    key_grad = matmul_tn(score_grad, query_rows) * SCORE_SCALE
    return (
        query_grad.astype(jnp.bfloat16),
        key_grad.astype(jnp.bfloat16),
        value_grad.astype(jnp.bfloat16),
    )


def width_forward(weight_set, row_in, same_seg, multiple):
    (
        query_weight,
        query_bias,
        key_weight,
        value_weight,
        value_bias,
        output_weight,
        output_bias,
        first_gain,
        first_shift,
        inner_weight,
        inner_bias,
        outer_weight,
        outer_bias,
        second_gain,
        second_shift,
    ) = weight_set
    head_count = HEADS * multiple // WIDTHS
    feat_width = head_count * DH
    hidden = FF * multiple // WIDTHS
    queries = (matmul(row_in, query_weight[:, :feat_width]) + query_bias[:feat_width]).astype(
        jnp.bfloat16
    )
    key_vals = matmul(row_in, key_weight[:, :feat_width]).astype(jnp.bfloat16)
    values = (matmul(row_in, value_weight[:, :feat_width]) + value_bias[:feat_width]).astype(
        jnp.bfloat16
    )
    head_outs, log_total = lax.map(
        lambda packed: head_forward(packed, same_seg),
        (
            split_heads(queries, head_count),
            split_heads(key_vals, head_count),
            split_heads(values, head_count),
        ),
    )
    attended = merge_heads(head_outs).astype(jnp.bfloat16)
    first_out, first_scaled, first_inverse = normalize(
        row_in + matmul(attended, output_weight[:feat_width]) + output_bias, first_gain, first_shift
    )
    first_low = first_out.astype(jnp.bfloat16)
    inner_pre = matmul(first_low, inner_weight[:, :hidden]) + inner_bias[:hidden]
    activated = jax.nn.gelu(inner_pre, approximate=False).astype(jnp.bfloat16)
    second_out, second_scaled, second_inverse = normalize(
        first_out + matmul(activated, outer_weight[:hidden]) + outer_bias, second_gain, second_shift
    )
    stored = (
        queries,
        key_vals,
        values,
        log_total,
        attended,
        first_scaled,
        first_inverse,
        first_low,
        inner_pre,
        activated,
        second_scaled,
        second_inverse,
    )
    return (second_out.astype(jnp.bfloat16), stored)


def feedforward_backward(weight_set, multiple, stored, upstream, grad_list):
    first_gain = weight_set[7]
    inner_weight = weight_set[9]
    outer_weight = weight_set[11]
    second_gain = weight_set[13]
    (
        queries,
        key_vals,
        values,
        log_total,
        attended,
        first_scaled,
        first_inverse,
        first_low,
        inner_pre,
        activated,
        second_scaled,
        second_inverse,
    ) = stored
    hidden = FF * multiple // WIDTHS
    grad_list = list(grad_list)
    grad_list[13] = grad_list[13] + jnp.sum(upstream * second_scaled, axis=0)
    grad_list[14] = grad_list[14] + jnp.sum(upstream, axis=0)
    second_back = norm_back(upstream, second_scaled, second_inverse, second_gain)
    outer_back = second_back.astype(jnp.bfloat16)
    grad_list[12] = grad_list[12] + jnp.sum(outer_back, axis=0, dtype=jnp.float32)
    grad_list[11] = grad_list[11].at[:hidden].add(matmul_tn(activated, outer_back))
    act_grad = matmul_nt(outer_back, outer_weight[:hidden])
    gelu_pull = jax.vjp(lambda pre_vals: jax.nn.gelu(pre_vals, approximate=False), inner_pre)[1]
    inner_back = gelu_pull(act_grad)[0].astype(jnp.bfloat16)
    grad_list[10] = grad_list[10].at[:hidden].add(jnp.sum(inner_back, axis=0, dtype=jnp.float32))
    grad_list[9] = grad_list[9].at[:, :hidden].add(matmul_tn(first_low, inner_back))
    first_back = second_back + matmul_nt(inner_back, inner_weight[:, :hidden])
    grad_list[7] = grad_list[7] + jnp.sum(first_back * first_scaled, axis=0)
    grad_list[8] = grad_list[8] + jnp.sum(first_back, axis=0)
    attn_back = norm_back(first_back, first_scaled, first_inverse, first_gain)
    return (attn_back, grad_list)


def attention_backward(weight_set, row_in, same_seg, multiple, stored, attn_back, grad_list):
    query_weight = weight_set[0]
    key_weight = weight_set[2]
    value_weight = weight_set[3]
    output_weight = weight_set[5]
    (
        queries,
        key_vals,
        values,
        log_total,
        attended,
        first_scaled,
        first_inverse,
        first_low,
        inner_pre,
        activated,
        second_scaled,
        second_inverse,
    ) = stored
    head_count = HEADS * multiple // WIDTHS
    feat_width = head_count * DH
    grad_list = list(grad_list)
    branch_back = attn_back.astype(jnp.bfloat16)
    grad_list[6] = grad_list[6] + jnp.sum(branch_back, axis=0, dtype=jnp.float32)
    grad_list[5] = grad_list[5].at[:feat_width].add(matmul_tn(attended, branch_back))
    attended_back = matmul_nt(branch_back, output_weight[:feat_width]).astype(jnp.bfloat16)
    query_heads, key_heads, value_heads = lax.map(
        lambda packed: head_backward(packed, same_seg),
        (
            split_heads(queries, head_count),
            split_heads(key_vals, head_count),
            split_heads(values, head_count),
            split_heads(attended_back, head_count),
            log_total,
        ),
    )
    query_back = merge_heads(query_heads)
    key_back = merge_heads(key_heads)
    value_back = merge_heads(value_heads)
    grad_list[1] = grad_list[1].at[:feat_width].add(jnp.sum(query_back, axis=0, dtype=jnp.float32))
    grad_list[4] = grad_list[4].at[:feat_width].add(jnp.sum(value_back, axis=0, dtype=jnp.float32))
    grad_list[0] = grad_list[0].at[:, :feat_width].add(matmul_tn(row_in, query_back))
    grad_list[2] = grad_list[2].at[:, :feat_width].add(matmul_tn(row_in, key_back))
    grad_list[3] = grad_list[3].at[:, :feat_width].add(matmul_tn(row_in, value_back))
    row_grad = (
        attn_back
        + matmul_nt(query_back, query_weight[:, :feat_width])
        + matmul_nt(key_back, key_weight[:, :feat_width])
        + matmul_nt(value_back, value_weight[:, :feat_width])
    )
    return (row_grad, grad_list)


def per_device(
    inputs,
    segments,
    out_grads,
    query_weight,
    query_bias,
    key_weight,
    value_weight,
    value_bias,
    output_weight,
    output_bias,
    first_gain,
    first_shift,
    inner_weight,
    inner_bias,
    outer_weight,
    outer_bias,
    second_gain,
    second_shift,
):
    gathered = (
        lax.all_gather(query_weight, ("dp", "fsdp"), axis=0, tiled=True),
        lax.all_gather(query_bias, ("dp", "fsdp"), axis=0, tiled=True),
        lax.all_gather(key_weight, ("dp", "fsdp"), axis=0, tiled=True),
        lax.all_gather(value_weight, ("dp", "fsdp"), axis=0, tiled=True),
        lax.all_gather(value_bias, ("dp", "fsdp"), axis=0, tiled=True),
        lax.all_gather(output_weight, ("dp", "fsdp"), axis=0, tiled=True),
        lax.all_gather(output_bias, ("dp", "fsdp"), axis=0, tiled=True),
        lax.all_gather(first_gain, ("dp", "fsdp"), axis=0, tiled=True),
        lax.all_gather(first_shift, ("dp", "fsdp"), axis=0, tiled=True),
        lax.all_gather(inner_weight, ("dp", "fsdp"), axis=0, tiled=True),
        lax.all_gather(inner_bias, ("dp", "fsdp"), axis=0, tiled=True),
        lax.all_gather(outer_weight, ("dp", "fsdp"), axis=0, tiled=True),
        lax.all_gather(outer_bias, ("dp", "fsdp"), axis=0, tiled=True),
        lax.all_gather(second_gain, ("dp", "fsdp"), axis=0, tiled=True),
        lax.all_gather(second_shift, ("dp", "fsdp"), axis=0, tiled=True),
    )
    row_index = 0
    row_seg = segments[row_index]
    same_seg = row_seg[:, None] == row_seg[None, :]
    same_list = [same_seg]
    width_outs = []
    width_stored = []
    for multiple in range(1, WIDTHS + 1):
        layer_out, stored = width_forward(gathered, inputs[row_index], same_seg, multiple)
        width_outs.append(layer_out)
        width_stored.append(stored)
    output_rows = [jnp.stack(width_outs)]
    stored_list = [width_stored]
    back_weights = (
        lax.all_gather(query_weight, ("dp", "fsdp"), axis=0, tiled=True),
        lax.all_gather(query_bias, ("dp", "fsdp"), axis=0, tiled=True),
        lax.all_gather(key_weight, ("dp", "fsdp"), axis=0, tiled=True),
        lax.all_gather(value_weight, ("dp", "fsdp"), axis=0, tiled=True),
        lax.all_gather(value_bias, ("dp", "fsdp"), axis=0, tiled=True),
        lax.all_gather(output_weight, ("dp", "fsdp"), axis=0, tiled=True),
        lax.all_gather(output_bias, ("dp", "fsdp"), axis=0, tiled=True),
        lax.all_gather(first_gain, ("dp", "fsdp"), axis=0, tiled=True),
        lax.all_gather(first_shift, ("dp", "fsdp"), axis=0, tiled=True),
        lax.all_gather(inner_weight, ("dp", "fsdp"), axis=0, tiled=True),
        lax.all_gather(inner_bias, ("dp", "fsdp"), axis=0, tiled=True),
        lax.all_gather(outer_weight, ("dp", "fsdp"), axis=0, tiled=True),
        lax.all_gather(outer_bias, ("dp", "fsdp"), axis=0, tiled=True),
        lax.all_gather(second_gain, ("dp", "fsdp"), axis=0, tiled=True),
        lax.all_gather(second_shift, ("dp", "fsdp"), axis=0, tiled=True),
    )
    grad_list = [jnp.zeros(weight_array.shape, jnp.float32) for weight_array in back_weights]
    row_index = 0
    row_total = jnp.zeros(inputs.shape[1:], jnp.float32)
    for multiple in range(1, WIDTHS + 1):
        upstream = out_grads[multiple - 1, row_index].astype(jnp.float32)
        stored = stored_list[row_index][multiple - 1]
        attn_back, grad_list = feedforward_backward(
            back_weights, multiple, stored, upstream, grad_list
        )
        row_grad, grad_list = attention_backward(
            back_weights,
            inputs[row_index],
            same_list[row_index],
            multiple,
            stored,
            attn_back,
            grad_list,
        )
        row_total = row_total + row_grad
    grad_rows = [row_total]
    reduced = (
        lax.psum_scatter(grad_list[0], ("dp", "fsdp"), scatter_dimension=0, tiled=True),
        lax.psum_scatter(grad_list[1], ("dp", "fsdp"), scatter_dimension=0, tiled=True),
        lax.psum_scatter(grad_list[2], ("dp", "fsdp"), scatter_dimension=0, tiled=True),
        lax.psum_scatter(grad_list[3], ("dp", "fsdp"), scatter_dimension=0, tiled=True),
        lax.psum_scatter(grad_list[4], ("dp", "fsdp"), scatter_dimension=0, tiled=True),
        lax.psum_scatter(grad_list[5], ("dp", "fsdp"), scatter_dimension=0, tiled=True),
        lax.psum_scatter(grad_list[6], ("dp", "fsdp"), scatter_dimension=0, tiled=True),
        lax.psum_scatter(grad_list[7], ("dp", "fsdp"), scatter_dimension=0, tiled=True),
        lax.psum_scatter(grad_list[8], ("dp", "fsdp"), scatter_dimension=0, tiled=True),
        lax.psum_scatter(grad_list[9], ("dp", "fsdp"), scatter_dimension=0, tiled=True),
        lax.psum_scatter(grad_list[10], ("dp", "fsdp"), scatter_dimension=0, tiled=True),
        lax.psum_scatter(grad_list[11], ("dp", "fsdp"), scatter_dimension=0, tiled=True),
        lax.psum_scatter(grad_list[12], ("dp", "fsdp"), scatter_dimension=0, tiled=True),
        lax.psum_scatter(grad_list[13], ("dp", "fsdp"), scatter_dimension=0, tiled=True),
        lax.psum_scatter(grad_list[14], ("dp", "fsdp"), scatter_dimension=0, tiled=True),
    )
    outputs = jnp.stack(output_rows, axis=1)
    input_grad = jnp.stack(grad_rows, axis=0)
    return (
        outputs,
        input_grad,
        reduced[0],
        reduced[1],
        reduced[2],
        reduced[3],
        reduced[4],
        reduced[5],
        reduced[6],
        reduced[7],
        reduced[8],
        reduced[9],
        reduced[10],
        reduced[11],
        reduced[12],
        reduced[13],
        reduced[14],
    )


def solution(mesh):
    placed = (
        P(("dp", "fsdp"), None, None),
        P(("dp", "fsdp"), None),
        P(None, ("dp", "fsdp"), None, None),
        P(("dp", "fsdp"), None),
        P(("dp", "fsdp")),
        P(("dp", "fsdp"), None),
        P(("dp", "fsdp"), None),
        P(("dp", "fsdp")),
        P(("dp", "fsdp"), None),
        P(("dp", "fsdp")),
        P(("dp", "fsdp")),
        P(("dp", "fsdp")),
        P(("dp", "fsdp"), None),
        P(("dp", "fsdp")),
        P(("dp", "fsdp"), None),
        P(("dp", "fsdp")),
        P(("dp", "fsdp")),
        P(("dp", "fsdp")),
    )
    return jax.shard_map(
        per_device,
        mesh=mesh,
        in_specs=placed,
        out_specs=(
            P(None, ("dp", "fsdp"), None, None),
            P(("dp", "fsdp"), None, None),
            P(("dp", "fsdp"), None),
            P(("dp", "fsdp")),
            P(("dp", "fsdp"), None),
            P(("dp", "fsdp"), None),
            P(("dp", "fsdp")),
            P(("dp", "fsdp"), None),
            P(("dp", "fsdp")),
            P(("dp", "fsdp")),
            P(("dp", "fsdp")),
            P(("dp", "fsdp"), None),
            P(("dp", "fsdp")),
            P(("dp", "fsdp"), None),
            P(("dp", "fsdp")),
            P(("dp", "fsdp")),
            P(("dp", "fsdp")),
        ),
        check_vma=False,
    )
```

profile of v0, /device:TPU:0, one launch (start us, length us, event | category | flops | bytes accessed | tf_op | source)
XLA Modules:
  0.0 1437.4 jit_solution(10282120461672007673)
XLA Ops:
  18.8 42.5 %all-reduce.28 = (bf16[768]{0:T(1024)(128)(2,1)S(1)}, bf16[768]{0:T(1024)(128)(2,1)S(1)}, bf16[768]{0:T(1024)(128)(2,1)S(1)}, bf16[768]{0:T(1024)(128)(2,1)S(1)}...) all-reduce(bf16[768]{0:T(1024)(128)(2,1)S(1)} %dynamic-update-slice, ...), channel_id=1, replica_groups=mesh['dp'=2,'fsdp'=16] {'dp','fsdp'}, use_global_device_ids=true, to_apply=%add.9 | all-reduce | flops 9216 | bytes 36864
  73.3 50.6 %all-gather.9.cloned.1.call-done = bf16[768,768]{1,0:T(8,128)(2,1)} async-done(((bf16[24,768]{1,0:T(8,128)(2,1)}), bf16[768,768]{1,0:T(8,128)(2,1)}) %all-gather.9.cloned.1.call-update) | async-done | bytes 1179664 | tf_op jit(solution)/shard_map/all_gather | solution.py:260
  127.8 51.9 %all-gather.11.cloned.1.call-done = bf16[768,768]{1,0:T(8,128)(2,1)} async-done(((bf16[24,768]{1,0:T(8,128)(2,1)}), bf16[768,768]{1,0:T(8,128)(2,1)}) %all-gather.11.cloned.1.call-update) | async-done | bytes 1179664 | tf_op jit(solution)/shard_map/all_gather | solution.py:261
  182.9 45.2 %while.160 = (s32[]{:T(128)}, bf16[12,512,64]{1,2,0:T(8,128)(2,1)}, f32[12,512]{1,0:T(8,128)}, bf16[12,512,64]{2,1,0:T(8,128)(2,1)}, bf16[12,512,64]{2,1,0:T(8,1...) while((s32[]{:T(128)}, bf16[12,512,64]{1,2,0:T(8,128)(2,1)}, ...), condition=%wide.region_27.28_spmd.clone, body=%wide.region_24.27_spmd.clone.sunk | while | flops 69467648 | bytes 3696745 | solution.py:110
  228.1 7.3 all-gather.13.cloned.1.call-done
  235.4 3.7 fusion.419
  246.1 22.3 %while.158 = (s32[]{:T(128)}, bf16[6,512,64]{1,2,0:T(8,128)(2,1)}, f32[6,512]{1,0:T(8,128)}, bf16[6,512,64]{2,1,0:T(8,128)(2,1)}, bf16[6,512,64]{2,1,0:T(8,128)(...) while((s32[]{:T(128)}, bf16[6,512,64]{1,2,0:T(8,128)(2,1)}, ...), condition=%wide.region_11.12_spmd.clone, body=%wide.region_8.11_spmd.clone.sunk | while | flops 69467648 | bytes 3696745 | solution.py:110
  283.6 2.7 fusion.299
  286.3 2.4 copy.88
  288.8 2.7 convolution_convert_fusion.7
  296.8 33.9 %while.159 = (s32[]{:T(128)}, bf16[9,512,64]{1,2,0:T(8,128)(2,1)}, f32[9,512]{1,0:T(8,128)}, bf16[9,512,64]{2,1,0:T(8,128)(2,1)}, bf16[9,512,64]{2,1,0:T(8,128)(...) while((s32[]{:T(128)}, bf16[9,512,64]{1,2,0:T(8,128)(2,1)}, ...), condition=%wide.region_19.20_spmd.clone, body=%wide.region_16.19_spmd.clone.sunk | while | flops 69467648 | bytes 3696745 | solution.py:110
  330.8 2.7 multiply_reduce_fusion.13
  334.4 14.3 while.157
  354.0 21.0 %multiply_convert_fusion.4 = (bf16[512,3072]{1,0:T(8,128)(2,1)}, f32[512,3072]{1,0:T(8,128)}, f32[512,3072]{1,0:T(8,128)}) fusion(f32[3072]{0:T(1024)S(1)} %copy-done.113, bf16[768,3072]{1,0:T(8,128)(2,1)} %all-gather.15.cloned.1.call-done, f32[512,768]{1,0:T(8,128)} %get-tuple-element.1412, f32[512]{0:T(512)S(1)} %add_rsqrt_fusion.1, ...), kind=kOutput, calls=%fused_computation.242 | convolution fusion | flops 2521694208 | bytes 22042624 | tf_op jit(solution)/shard_map/dot_general | solution.py:18
  375.0 6.6 fusion.420
  382.4 8.0 multiply_convert_fusion.6
  393.4 4.5 multiply_convert_fusion.7
  400.3 14.5 %multiply_convert_fusion.5 = (bf16[512,2304]{1,0:T(8,128)(2,1)S(1)}, f32[512,2304]{1,0:T(8,128)}, f32[512,2304]{1,0:T(8,128)}) fusion(f32[2304]{0:T(1024)S(1)} %copy-done.114, bf16[768,3072]{1,0:T(8,128)(2,1)S(1)} %bitcast.778, f32[512,768]{1,0:T(8,128)S(1)} %copy-done.14, f32[512]{0:T(512)S(1)} %add_rsqrt_fusion.3, f32[512]{0:T(512)S(1)} %broadcast_multiply_fusion.19, ...), kind=kOutput, calls=%fused_computation.265 | convolution fusion | flops 1891762176 | bytes 16932864 | tf_op jit(solution)/shard_map/dot_general | solution.py:18
  417.9 2.9 fusion.270
  420.8 4.0 convert_reduce_fusion.10
  424.8 3.5 convert_reduce_fusion.9
  428.3 3.0 convert_reduce_fusion.2
  434.7 3.6 multiply_reduce_fusion.7
  438.3 6.7 convert_reduce_fusion.1
  447.1 9.3 convert_reduce_fusion
  456.4 9.0 convert_reduce_fusion.15
  465.5 3.2 convert_reduce_fusion.14
  474.0 91.8 %while.164 = (s32[]{:T(128)}, bf16[12,512,64]{1,2,0:T(8,128)(2,1)S(1)}, bf16[12,512,64]{1,2,0:T(8,128)(2,1)}, bf16[12,512,64]{1,2,0:T(8,128)(2,1)S(1)}, bf16[12,...) while((s32[]{:T(128)}, ...), condition=%wide.region_59.60_spmd.clone, body=%wide.region_57.59_spmd.clone.sunk | while | flops 170556928 | bytes 8866937 | solution.py:210
  566.8 3.1 convolution_convert_fusion.6
  572.2 76.2 %while.163 = (s32[]{:T(128)}, bf16[9,512,64]{1,2,0:T(8,128)(2,1)S(1)}, bf16[9,512,64]{1,2,0:T(8,128)(2,1)}, bf16[9,512,64]{1,2,0:T(8,128)(2,1)}, bf16[9,512,64]{...) while((s32[]{:T(128)}, ...), condition=%wide.region_52.53_spmd.clone, body=%wide.region_50.52_spmd.clone.sunk | while | flops 170556928 | bytes 8998009 | solution.py:210
  648.4 2.6 convolution_convert_fusion.8
  652.4 44.7 %while.162 = (s32[]{:T(128)}, bf16[6,512,64]{1,2,0:T(8,128)(2,1)S(1)}, bf16[6,512,64]{1,2,0:T(8,128)(2,1)}, bf16[6,512,64]{1,2,0:T(8,128)(2,1)}, bf16[6,512,64]{...) while((s32[]{:T(128)}, ...), condition=%wide.region_45.46_spmd.clone, body=%wide.region_43.45_spmd.clone.sunk | while | flops 170556928 | bytes 8998009 | solution.py:210
  699.3 24.2 %while.161 = (s32[]{:T(128)}, bf16[3,512,64]{1,2,0:T(8,128)(2,1)}, bf16[3,512,64]{1,2,0:T(8,128)(2,1)}, bf16[3,512,64]{1,2,0:T(8,128)(2,1)}, bf16[3,512,64]{2,1,...) while((s32[]{:T(128)}, bf16[3,512,64]{1,2,0:T(8,128)(2,1)}, ...), condition=%wide.region_38.39_spmd.clone, body=%wide.region_36.38_spmd.clone.sunk | while | flops 170556928 | bytes 8998009 | solution.py:210
  731.5 3.0 copy.109
  742.4 3.1 copy.111
  753.4 3.1 copy.113
  770.8 3.1 fusion.201
  774.0 4.5 fusion.192
  778.5 5.7 convolution_add_fusion.1
  790.7 2.5 fusion.193
  793.2 5.3 convolution_add_fusion
  823.0 41.4 %all-reduce.27 = (f32[768]{0:T(1024)}, f32[768]{0:T(1024)}, f32[768]{0:T(1024)}, f32[768]{0:T(1024)}, f32[768]{0:T(1024)}, /*index=5*/f32[3072]{0:T(1024)}, f32[768]{0:T(1024)}, f32[768]{0:T(1024)}, f32[768]{0:T(1024)}) all-reduce(f32[768]{0:T(1024)S(1)} %add.867, ...), channel_id=3, replica_groups=mesh['dp'=2,'fsdp'=16] {'dp','fsdp'}, use_global_device_ids=true, to_apply=%region_68.69.clone | all-reduce | flops 9216 | bytes 73728
  890.3 2.9 add_bitcast_fusion
  893.3 44.5 %reduce-scatter.21.cloned.1.call-done = f32[24,768]{1,0:T(8,128)} async-done(((f32[768,768]{1,0:T(8,128)}), f32[24,768]{1,0:T(8,128)}) %reduce-scatter.21.cloned.1.call-update) | async-done | bytes 73744
  937.8 104.6 %reduce-scatter.23.cloned.1.call-done = f32[24,768]{1,0:T(8,128)} async-done(((f32[768,768]{1,0:T(8,128)}), f32[24,768]{1,0:T(8,128)}) %reduce-scatter.23.cloned.1.call-update) | async-done | bytes 73744
  1042.4 104.4 %reduce-scatter.13.cloned.1.call-done = f32[24,768]{1,0:T(8,128)} async-done(((f32[768,768]{1,0:T(8,128)}), f32[24,768]{1,0:T(8,128)}) %reduce-scatter.13.cloned.1.call-update) | async-done | bytes 73744 | tf_op jit(solution)/shard_map/reduce_scatter | solution.py:329
  1146.8 141.8 %reduce-scatter.15.cloned.1.call-done = f32[24,3072]{1,0:T(8,128)} async-done(((f32[768,3072]{1,0:T(8,128)}), f32[24,3072]{1,0:T(8,128)}) %reduce-scatter.15.cloned.1.call-update) | async-done | bytes 294928 | tf_op jit(solution)/shard_map/reduce_scatter | solution.py:333
  1288.5 141.5 %reduce-scatter.17.cloned.1.call-done = f32[96,768]{1,0:T(8,128)} async-done(((f32[3072,768]{1,0:T(8,128)}), f32[96,768]{1,0:T(8,128)}) %reduce-scatter.17.cloned.1.call-update) | async-done | bytes 294928 | tf_op jit(solution)/shard_map/reduce_scatter | solution.py:335
  (884 shorter events, 535.9 us)
Async XLA Ops:
  7.2 62.0 %all-gather.7.cloned.1.call-start = ((), (), s32[]{:S(2)}) async-start(), calls=%async_computation.6 | async-start | bytes 1216512 | tf_op jit(solution)/shard_map/all_gather | solution.py:258
  7.9 115.9 %all-gather.9.cloned.1.call-start = ((), (), s32[]{:S(2)}) async-start(), calls=%async_computation.7 | async-start | bytes 1216512 | tf_op jit(solution)/shard_map/all_gather | solution.py:260
  8.7 171.0 %all-gather.11.cloned.1.call-start = ((), (), s32[]{:S(2)}) async-start(), calls=%async_computation.8 | async-start | bytes 1216512 | tf_op jit(solution)/shard_map/all_gather | solution.py:261
  9.4 226.0 %all-gather.13.cloned.1.call-start = ((), (), s32[]{:S(2)}) async-start(), calls=%async_computation.9 | async-start | bytes 1216512 | tf_op jit(solution)/shard_map/all_gather | solution.py:263
  10.0 344.0 %all-gather.15.cloned.1.call-start = ((), (), s32[]{:S(2)}) async-start(), calls=%async_computation.10 | async-start | bytes 4866048 | tf_op jit(solution)/shard_map/all_gather | solution.py:267
  10.6 364.4 %all-gather.17.cloned.1.call-start = ((), (), s32[]{:S(2)}) async-start(), calls=%async_computation.11 | async-start | bytes 4866048 | tf_op jit(solution)/shard_map/all_gather | solution.py:269
  11.1 882.1 %reduce-scatter.19.cloned.1.call-start = ((), (), s32[]{:S(2)}) async-start(), calls=%async_computation.15 | async-start | bytes 2433024
  68.0 167.4 %copy-start.102 = (f32[768]{0:T(1024)}, f32[768]{0:T(1024)S(1)}, u32[]{:S(2)}) copy-start(f32[768]{0:T(1024)S(1)} %convert_element_type.415) | copy-start | bytes 9220
  71.8 52.1 %copy-start = (bf16[1,512,768]{2,1,0:T(8,128)(2,1)S(1)}, bf16[1,512,768]{2,1,0:T(8,128)(2,1)}, u32[]{:S(2)}) copy-start(bf16[1,512,768]{2,1,0:T(8,128)(2,1)} %param.124) | copy-start | bytes 2359300
  228.1 11.0 copy-start.59
  271.5 163.2 %copy-start.8 = (f32[512,768]{1,0:T(8,128)}, f32[512,768]{1,0:T(8,128)S(1)}, u32[]{:S(2)}) copy-start(f32[512,768]{1,0:T(8,128)S(1)} %get-tuple-element.1417) | copy-start | bytes 4718596
  278.2 5.5 copy-start.124
  334.4 14.3 copy-start.39
  353.8 111.6 %copy-start.104 = (f32[512]{0:T(512)}, f32[512]{0:T(512)S(1)}, u32[]{:S(2)}) copy-start(f32[512]{0:T(512)S(1)} %add_rsqrt_fusion.1) | copy-start | bytes 6148
  353.9 111.6 %copy-start.111 = (f32[512]{0:T(512)}, f32[512]{0:T(512)S(1)}, u32[]{:S(2)}) copy-start(f32[512]{0:T(512)S(1)} %add_rsqrt_fusion.5) | copy-start | bytes 6148
  353.9 102.5 %copy-start.125 = (f32[512]{0:T(512)}, f32[512]{0:T(512)S(1)}, u32[]{:S(2)}) copy-start(f32[512]{0:T(512)S(1)} %add_rsqrt_fusion.7) | copy-start | bytes 6148
  353.9 111.5 %copy-start.106 = (f32[512]{0:T(512)}, f32[512]{0:T(512)S(1)}, u32[]{:S(2)}) copy-start(f32[512]{0:T(512)S(1)} %add_rsqrt_fusion.3) | copy-start | bytes 6148
  353.9 21.1 %copy-start.122 = (f32[768]{0:T(1024)S(1)}, f32[768]{0:T(1024)}, u32[]{:S(2)}) copy-start(f32[768]{0:T(1024)} %convert_element_type.421) | copy-start | bytes 9220
  375.0 7.0 slice-start
  375.0 7.0 slice-start.1
  381.7 8.7 slice-start.2
  382.4 8.0 slice-start.3
  424.8 9.9 copy-start.35
  424.8 31.6 %copy-start.28 = (f32[512,768]{1,0:T(8,128)}, f32[512,768]{1,0:T(8,128)S(1)}, u32[]{:S(2)}) copy-start(f32[512,768]{1,0:T(8,128)S(1)} %get-tuple-element.1385) | copy-start | bytes 4718596
  428.3 16.7 %copy-start.30 = (f32[512,768]{1,0:T(8,128)}, f32[512,768]{1,0:T(8,128)S(1)}, u32[]{:S(2)}) copy-start(f32[512,768]{1,0:T(8,128)S(1)} %get-tuple-element.1390) | copy-start | bytes 4718596
  447.1 9.3 copy-start.11
  447.1 9.3 copy-start.130
  456.4 9.1 copy-start.60
  456.4 9.1 copy-start.9
  456.4 9.1 copy-start.82
  468.7 290.6 %copy-start.4 = (f32[512,768]{1,0:T(8,128)}, f32[512,768]{1,0:T(8,128)S(1)}, u32[]{:S(2)}) copy-start(f32[512,768]{1,0:T(8,128)S(1)} %get-tuple-element.1353) | copy-start | bytes 4718596
  565.9 185.2 %copy-start.23 = (bf16[12,512,64]{1,2,0:T(8,128)(2,1)}, bf16[12,512,64]{1,2,0:T(8,128)(2,1)S(1)}, u32[]{:S(2)}) copy-start(bf16[12,512,64]{1,2,0:T(8,128)(2,1)S(1)} %get-tuple-element.908) | copy-start | bytes 2359300
  699.3 24.2 %copy-start.1 = (bf16[1,512,768]{2,1,0:T(8,128)(2,1)S(1)}, bf16[1,512,768]{2,1,0:T(8,128)(2,1)}, u32[]{:S(2)}) copy-start(bf16[1,512,768]{2,1,0:T(8,128)(2,1)} %param.124) | copy-start | bytes 2359300
  734.5 203.2 %reduce-scatter.21.cloned.1.call-start = ((), (), s32[]{:S(2)}) async-start(), calls=%async_computation.16 | async-start | bytes 2433024
  745.5 296.8 %reduce-scatter.23.cloned.1.call-start = ((), (), s32[]{:S(2)}) async-start(), calls=%async_computation.17 | async-start | bytes 2433024
  756.5 390.3 %reduce-scatter.13.cloned.1.call-start = ((), (), s32[]{:S(2)}) async-start(), calls=%async_computation.12 | async-start | bytes 2433024 | tf_op jit(solution)/shard_map/reduce_scatter | solution.py:329
  765.6 523.0 %reduce-scatter.15.cloned.1.call-start = ((), (), s32[]{:S(2)}) async-start(), calls=%async_computation.13 | async-start | bytes 9732096 | tf_op jit(solution)/shard_map/reduce_scatter | solution.py:333
  774.0 4.5 copy-start.12
  774.0 4.5 copy-start.61
  784.2 645.8 %reduce-scatter.17.cloned.1.call-start = ((), (), s32[]{:S(2)}) async-start(), calls=%async_computation.14 | async-start | bytes 9732096 | tf_op jit(solution)/shard_map/reduce_scatter | solution.py:335
  800.8 5.6 copy-start.80
  800.8 5.8 copy-start.58
  800.8 6.6 copy-start.46
  801.5 6.7 copy-start.24
  804.3 71.5 %copy-start.21 = (bf16[768,768]{1,0:T(8,128)(2,1)S(1)}, bf16[768,768]{1,0:T(8,128)(2,1)}, u32[]{:S(2)}) copy-start(bf16[768,768]{1,0:T(8,128)(2,1)} %all-gather.11.cloned.1.call-done) | copy-start | bytes 3538948
  808.2 69.4 %copy-start.78 = (bf16[3,512,64]{1,2,0:T(8,128)(2,1)S(1)}, bf16[3,512,64]{1,2,0:T(8,128)(2,1)}, u32[]{:S(2)}) copy-start(bf16[3,512,64]{1,2,0:T(8,128)(2,1)} %get-tuple-element.894) | copy-start | bytes 589828
  864.4 12.8 copy-start.52
  864.4 12.8 copy-start.97
  (103 other events, 183.6 us)
Sparse Core Ops, SparseCore 0:
  10.9 56.8 all-gather.6
  70.7 53.1 all-gather.8
  126.8 52.8 all-gather.10
  182.4 52.9 all-gather.12
  238.2 62.5 all-gather.14
  303.5 61.8 all-gather.16
  734.7 98.5 reduce-scatter.18
  839.1 98.6 reduce-scatter.20
  943.6 98.6 reduce-scatter.22
  1048.1 98.6 reduce-scatter.12
  1153.3 135.2 reduce-scatter.14
  1294.9 135.1 reduce-scatter.16
where the time goes:
time: 1460 us; the launch traced here: 1440 us
  waiting for transfers between devices  650 us (45%)
  matrix products  470 us (32%)
  local copies, waits for them, and re-layouts  153 us (10%)
  blocking collectives  83.9 us (6%)
  other arithmetic  62.2 us (4%)
  between operations  16.4 us (1%)
    dot_general x114, matrix products, matmul_nt(): lax.dot_general(left, right, (((1,), (1,)), ((), ())), preferred_element_...  173 us
    dot_general x84, matrix products, matmul(): return jnp.dot(left, right, preferred_element_type=jnp.float32)  155 us
    unnamed x15, waiting for transfers between devices  153 us
    reduce_scatter x1, waiting for transfers between devices, per_device(): lax.psum_scatter(grad_list[9], ('dp', 'fsdp'), scatter_dimension=0, tiled...  142 us
    dot_general x84, matrix products, matmul_tn(): lax.dot_general(left, right, (((0,), (0,)), ((), ())), preferred_element_...  142 us
    reduce_scatter x1, waiting for transfers between devices, per_device(): lax.psum_scatter(grad_list[11], ('dp', 'fsdp'), scatter_dimension=0, tile...  142 us
    reduce_scatter x1, waiting for transfers between devices, per_device(): lax.psum_scatter(grad_list[5], ('dp', 'fsdp'), scatter_dimension=0, tiled...  104 us
    unnamed x2, blocking collectives  83.9 us
  transfers between devices with their start and end apart: 12, of which 8 were waited for; matrix products, arithmetic and copies ran while one was open for 21% of the time, Pallas kernels for 0%

commit v1 on v0

v1 whole, which is shorter than its diff:
```python
import functools

import jax
import jax.numpy as jnp
from jax import lax
from jax.experimental import pallas as pl
from jax.experimental.pallas import tpu as pltpu
from jax.sharding import PartitionSpec as P

HEADS = 12
DH = 64
WIDTHS = 4
EPSILON = 1e-12
SCORE_SCALE = 0.125
MASKED = -1000000000.0
BF = jnp.bfloat16
F32 = jnp.float32
AXES = ("dp", "fsdp")
EXTRA = 128


def dot(a, b):
    return jnp.dot(a, b, preferred_element_type=F32)


def dot_tn(a, b):
    return lax.dot_general(a, b, (((0,), (0,)), ((), ())), preferred_element_type=F32)


def dot_nt(a, b):
    return lax.dot_general(a, b, (((1,), (1,)), ((), ())), preferred_element_type=F32)


def attn_fwd_kernel(q_ref, k_ref, v_ref, segc_ref, segr_ref, o_ref, lse_ref):
    q = q_ref[...]
    k = k_ref[...]
    v = v_ref[...]
    lane = lax.broadcasted_iota(jnp.int32, q.shape, 1)
    low = lane < DH
    zero = jnp.zeros_like(q)
    same = segc_ref[...] == segr_ref[...]
    outs = []
    lses = []
    for half in range(2):
        qh = jnp.where(low if half == 0 else ~low, q, zero)
        s = jnp.where(same, dot_nt(qh, k) * SCORE_SCALE, MASKED)
        m = jnp.max(s, axis=-1, keepdims=True)
        e = jnp.exp(s - m)
        total = jnp.sum(e, axis=-1, keepdims=True)
        p = (e * (1.0 / total)).astype(BF)
        outs.append(dot(p, v))
        lses.append(m + jnp.log(total))
    o_ref[...] = jnp.where(low, outs[0], outs[1]).astype(BF)
    lse_ref[...] = jnp.where(low, lses[0], lses[1])


def attn_bwd_kernel(q_ref, k_ref, v_ref, g_ref, segc_ref, segr_ref, lse_ref, dq_ref, dk_ref, dv_ref):
    q = q_ref[...]
    k = k_ref[...]
    v = v_ref[...]
    g = g_ref[...]
    lane = lax.broadcasted_iota(jnp.int32, q.shape, 1)
    low = lane < DH
    zero = jnp.zeros_like(q)
    same = segc_ref[...] == segr_ref[...]
    res = []
    for half in range(2):
        mine = low if half == 0 else ~low
        qh = jnp.where(mine, q, zero)
        gh = jnp.where(mine, g, zero)
        s = jnp.where(same, dot_nt(qh, k) * SCORE_SCALE, MASKED)
        p = jnp.exp(s - lse_ref[:, half * DH : half * DH + 1])
        dp = dot_nt(gh, v)
        ds = (p * (dp - jnp.sum(p * dp, axis=-1, keepdims=True))).astype(BF)
        res.append((dot(ds, k), dot_tn(ds, q), dot_tn(p.astype(BF), g)))
    dq_ref[...] = (jnp.where(low, res[0][0], res[1][0]) * SCORE_SCALE).astype(BF)
    dk_ref[...] = (jnp.where(low, res[0][1], res[1][1]) * SCORE_SCALE).astype(BF)
    dv_ref[...] = jnp.where(low, res[0][2], res[1][2]).astype(BF)


def attn_forward(qkv, segc, segr):
    seq = qkv.shape[0]
    pairs = HEADS // 2
    block = lambda off: pl.BlockSpec((seq, 2 * DH), lambda i: (0, i + off))
    return pl.pallas_call(
        attn_fwd_kernel,
        grid=(pairs,),
        in_specs=[block(0), block(pairs), block(2 * pairs),
                  pl.BlockSpec((seq, 1), lambda i: (0, 0)), pl.BlockSpec((1, seq), lambda i: (0, 0))],
        out_specs=[block(0), block(0)],
        out_shape=[jax.ShapeDtypeStruct((seq, HEADS * DH), BF), jax.ShapeDtypeStruct((seq, HEADS * DH), F32)],
        compiler_params=pltpu.CompilerParams(vmem_limit_bytes=48 << 20),
        name="attn_fwd",
    )(qkv, qkv, qkv, segc, segr)


def attn_backward(qkv, g, segc, segr, lse):
    seq = qkv.shape[0]
    pairs = HEADS // 2
    block = lambda off: pl.BlockSpec((seq, 2 * DH), lambda i: (0, i + off))
    out = jax.ShapeDtypeStruct((seq, HEADS * DH), BF)
    return pl.pallas_call(
        attn_bwd_kernel,
        grid=(pairs,),
        in_specs=[block(0), block(pairs), block(2 * pairs), block(0),
                  pl.BlockSpec((seq, 1), lambda i: (0, 0)), pl.BlockSpec((1, seq), lambda i: (0, 0)), block(0)],
        out_specs=[block(0)] * 3,
        out_shape=[out] * 3,
        compiler_params=pltpu.CompilerParams(vmem_limit_bytes=48 << 20),
        name="attn_bwd",
    )(qkv, qkv, qkv, g, segc, segr, lse)


def normalize(hidden):
    center = hidden - jnp.mean(hidden, axis=-1, keepdims=True)
    inverse = lax.rsqrt(jnp.mean(center * center, axis=-1, keepdims=True) + EPSILON)
    return center * inverse, inverse


def norm_back(upstream, scaled, inverse, gain):
    tg = upstream * gain
    return inverse * (tg - jnp.mean(tg, axis=-1, keepdims=True) - scaled * jnp.mean(tg * scaled, axis=-1, keepdims=True))


def gelu_parts(x):
    phi = 0.5 * (1.0 + lax.erf(x * 0.7071067811865476))
    slope = phi + x * (jnp.exp(-0.5 * x * x) * 0.3989422804014327)
    return (x * phi).astype(BF), slope.astype(BF)


def per_device(inputs, segments, out_grads, wq, bq, wk, wv, bv, wo, bo, g1, s1, wi, bi, wu, bu, g2, s2):
    rows = wq.shape[0]
    dim = wq.shape[1]
    ff = wi.shape[1]
    feat = dim // WIDTHS
    hid = ff // WIDTHS
    small = jnp.concatenate(
        [jnp.stack([bq, bv, bo, g1, s1, bu, g2, s2], axis=1), bi.reshape(rows, ff // dim)], axis=1
    )
    nsmall = small.shape[1]
    small = jnp.pad(small, ((0, 0), (0, EXTRA - nsmall)))
    packed = jnp.concatenate([wq, wk, wv, wo, wi, wu.reshape(rows, ff), small], axis=1)
    full = lax.all_gather(packed, AXES, axis=0, tiled=True)
    wqkv = full[:, : 3 * dim]
    wo_f = full[:, 3 * dim : 4 * dim]
    wi_f = full[:, 4 * dim : 4 * dim + ff]
    wu_f = full[:, 4 * dim + ff : 4 * dim + 2 * ff].reshape(ff, dim)
    sm = full[:, 4 * dim + 2 * ff :].astype(F32)
    vec = sm[:, :8].T
    bq_f, bv_f, bo_f, g1_f, s1_f, bu_f, g2_f, s2_f = [vec[i] for i in range(8)]
    bi_f = sm[:, 8 : 8 + ff // dim].reshape(ff)

    x = inputs[0]
    xf = x.astype(F32)
    seg = segments[0]
    segc, segr = seg[:, None], seg[None, :]
    bqkv = jnp.concatenate([bq_f, jnp.zeros_like(bq_f), bv_f])
    qkv = (dot(x, wqkv) + bqkv).astype(BF)
    att, lse = attn_forward(qkv, segc, segr)

    branch = jnp.zeros(x.shape, F32)
    outs = []
    acts = []
    slopes = []
    lows = []
    back = []
    for k in range(WIDTHS):
        branch = branch + dot(att[:, feat * k : feat * (k + 1)], wo_f[feat * k : feat * (k + 1)])
        scaled1, inv1 = normalize(xf + branch + bo_f)
        first = scaled1 * g1_f + s1_f
        low = first.astype(BF)
        pre = dot(low, wi_f[:, : hid * (k + 1)]) + bi_f[: hid * (k + 1)]
        act, slope = gelu_parts(pre)
        scaled2, inv2 = normalize(first + dot(act, wu_f[: hid * (k + 1)]) + bu_f)
        outs.append((scaled2 * g2_f + s2_f).astype(BF))
        back.append((scaled1, inv1, scaled2, inv2))
        lows.append(low)
        acts.append(act)
        slopes.append(slope)

    obs = []
    ibs = []
    ab_suffix = [None] * WIDTHS
    d_g1 = d_s1 = d_g2 = d_s2 = d_bu = jnp.zeros((dim,), F32)
    bbs = []
    attn_total = jnp.zeros(x.shape, F32)
    for k in range(WIDTHS):
        scaled1, inv1, scaled2, inv2 = back[k]
        up = out_grads[k, 0].astype(F32)
        d_g2 = d_g2 + jnp.sum(up * scaled2, axis=0)
        d_s2 = d_s2 + jnp.sum(up, axis=0)
        sb = norm_back(up, scaled2, inv2, g2_f)
        ob = sb.astype(BF)
        d_bu = d_bu + jnp.sum(ob, axis=0, dtype=F32)
        ib = (dot_nt(ob, wu_f[: hid * (k + 1)]) * slopes[k].astype(F32)).astype(BF)
        fb = sb + dot_nt(ib, wi_f[:, : hid * (k + 1)])
        d_g1 = d_g1 + jnp.sum(fb * scaled1, axis=0)
        d_s1 = d_s1 + jnp.sum(fb, axis=0)
        ab = norm_back(fb, scaled1, inv1, g1_f)
        attn_total = attn_total + ab
        bbs.append(ab)
        obs.append(ob)
        ibs.append(ib)
    suffix = None
    for k in range(WIDTHS - 1, -1, -1):
        suffix = bbs[k] if suffix is None else suffix + bbs[k]
        ab_suffix[k] = suffix.astype(BF)
    d_bo = jnp.sum(attn_total, axis=0)
    d_wo = jnp.concatenate(
        [dot_tn(att[:, feat * k : feat * (k + 1)], ab_suffix[k]) for k in range(WIDTHS)], axis=0
    )
    att_back = jnp.concatenate(
        [dot_nt(ab_suffix[k], wo_f[feat * k : feat * (k + 1)]) for k in range(WIDTHS)], axis=1
    ).astype(BF)

    d_wi = []
    d_wu = []
    d_bi = []
    for j in range(WIDTHS):
        cols = slice(hid * j, hid * (j + 1))
        ib_j = jnp.concatenate([ibs[k][:, cols] for k in range(j, WIDTHS)], axis=0)
        act_j = jnp.concatenate([acts[k][:, cols] for k in range(j, WIDTHS)], axis=0)
        low_j = jnp.concatenate(lows[j:], axis=0)
        ob_j = jnp.concatenate(obs[j:], axis=0)
        d_wi.append(dot_tn(low_j, ib_j))
        d_wu.append(dot_tn(act_j, ob_j))
        d_bi.append(jnp.sum(ib_j, axis=0, dtype=F32))
    d_wi = jnp.concatenate(d_wi, axis=1)
    d_wu = jnp.concatenate(d_wu, axis=0)
    d_bi = jnp.concatenate(d_bi)

    dq, dk, dv = attn_backward(qkv, att_back, segc, segr, lse)
    dqkv = jnp.concatenate([dq, dk, dv], axis=1)
    d_wqkv = dot_tn(x, dqkv)
    x_grad = attn_total + dot_nt(dqkv, wqkv)
    d_bq = jnp.sum(dq, axis=0, dtype=F32)
    d_bv = jnp.sum(dv, axis=0, dtype=F32)

    d_small = jnp.concatenate(
        [jnp.stack([d_bq, d_bv, d_bo, d_g1, d_s1, d_bu, d_g2, d_s2], axis=1), d_bi.reshape(dim, ff // dim)], axis=1
    )
    d_small = jnp.pad(d_small, ((0, 0), (0, EXTRA - nsmall)))
    d_packed = jnp.concatenate(
        [d_wqkv.astype(BF), d_wo.astype(BF), d_wi.astype(BF), d_wu.astype(BF).reshape(dim, ff), d_small.astype(BF)],
        axis=1,
    )
    red = lax.psum_scatter(d_packed, AXES, scatter_dimension=0, tiled=True).astype(F32)
    rs = red[:, 4 * dim + 2 * ff :]
    vecs = [rs[:, i] for i in range(8)]
    r_bi = rs[:, 8 : 8 + ff // dim].reshape(-1)
    return (
        jnp.stack(outs)[:, None],
        x_grad[None],
        red[:, :dim],
        vecs[0],
        red[:, dim : 2 * dim],
        red[:, 2 * dim : 3 * dim],
        vecs[1],
        red[:, 3 * dim : 4 * dim],
        vecs[2],
        vecs[3],
        vecs[4],
        red[:, 4 * dim : 4 * dim + ff],
        r_bi,
        red[:, 4 * dim + ff : 4 * dim + 2 * ff].reshape(-1, dim),
        vecs[5],
        vecs[6],
        vecs[7],
    )


def solution(mesh):
    mat = P(AXES, None)
    vec = P(AXES)
    params = (mat, vec, mat, mat, vec, mat, vec, vec, vec, mat, vec, mat, vec, vec, vec)
    return jax.shard_map(
        per_device,
        mesh=mesh,
        in_specs=(P(AXES, None, None), P(AXES, None), P(None, AXES, None, None)) + params,
        out_specs=(P(None, AXES, None, None), P(AXES, None, None)) + params,
        check_vma=False,
    )
```

time: 1460 us -> 591 us (0.40); the launches traced: 1440 us -> 584 us
  waiting for transfers between devices: 650 us -> 252 us
  matrix products: 470 us -> 121 us
  blocking collectives: 83.9 us -> 0 us
  local copies, waits for them, and re-layouts: 153 us -> 128 us
  Pallas kernels: 0 us -> 24.7 us
  other arithmetic: 62.2 us -> 42.2 us
    reduce_scatter x3 -> x0, waiting for transfers between devices: 388 us -> none  [the longest x1 142 us: per_device(): lax.psum_scatter(grad_list[9], ('dp', 'fsdp'), scatter_dimension=0, tiled...]
    dot_general x282 -> x39, matrix products: 470 us -> 121 us  [the longest x13 45.2 us: dot_nt(): lax.dot_general(a, b, (((1,), (1,)), ((), ())), preferred_element_type=F32)]
    unnamed x2 -> x0, blocking collectives: 83.9 us -> none
    dynamic_update_slice x30 -> x0, local copies, waits for them, and re-layouts: 40.2 us -> none  [width_forward(): lax.map(lambda packed: head_forward(packed, same_seg), (split_heads(queri...]
    slice x0 -> x19, local copies, waits for them, and re-layouts: none -> 39 us  [the longest x6 24.7 us: per_device(): scaled2, inv2 = normalize(first + dot(act, wu_f[:hid * (k + 1)]) + bu_f)]
    pallas_call x0 -> x2, Pallas kernels: none -> 24.7 us  [the longest x1 15.3 us: attn_backward(): pl.pallas_call(attn_bwd_kernel, grid=(pairs,), in_specs=[block(0), block(...]
    dynamic_slice x30 -> x0, local copies, waits for them, and re-layouts: 21.7 us -> none  [attention_backward(): lax.map(lambda packed: head_backward(packed, same_seg), (split_heads(quer...]
    unnamed x299 -> x253, local copies, waits for them, and re-layouts: 58.4 us -> 38.1 us
  transfers between devices with their start and end apart: 12 -> 2, of which waited for: 8 -> 2; matrix products, arithmetic and copies ran while one was open for 21% -> 2% of each run, Pallas kernels for 0% -> 0%
where the time goes in v1:
time: 591 us; the launch traced here: 584 us
  waiting for transfers between devices  252 us (43%)
  local copies, waits for them, and re-layouts  128 us (22%)
  matrix products  121 us (20%)
  other arithmetic  42.2 us (7%)
  Pallas kernels  24.7 us (4%)
  between operations  15.7 us (3%)
    unnamed x3, waiting for transfers between devices  149 us
    all_gather x1, waiting for transfers between devices, per_device(): full = lax.all_gather(packed, AXES, axis=0, tiled=True)  103 us
    dot_general x13, matrix products, dot_nt(): lax.dot_general(a, b, (((1,), (1,)), ((), ())), preferred_element_type=F32)  45.2 us
    dot_general x13, matrix products, dot(): return jnp.dot(a, b, preferred_element_type=F32)  39 us
    unnamed x253, local copies, waits for them, and re-layouts  38.1 us
    dot_general x13, matrix products, dot_tn(): lax.dot_general(a, b, (((0,), (0,)), ((), ())), preferred_element_type=F32)  36.8 us
    slice x6, local copies, waits for them, and re-layouts, per_device(): scaled2, inv2 = normalize(first + dot(act, wu_f[:hid * (k + 1)]) + bu_f)  24.7 us
    pallas_call x1, Pallas kernels, attn_backward(): pl.pallas_call(attn_bwd_kernel, grid=(pairs,), in_specs=[block(0), block(...  15.3 us
  transfers between devices with their start and end apart: 2, of which 2 were waited for; matrix products, arithmetic and copies ran while one was open for 2% of the time, Pallas kernels for 0%

profile of v1, /device:TPU:0, one launch (start us, length us, event | category | flops | bytes accessed | tf_op | source)
XLA Modules:
  0.0 583.7 jit_solution(15611392986340426692)
XLA Ops:
  23.1 103.0 %all-gather.2.cloned.1.call-done = bf16[768,9344]{1,0:T(8,128)(2,1)} async-done(((bf16[24,9344]{1,0:T(8,128)(2,1)}), bf16[768,9344]{1,0:T(8,128)(2,1)}) %all-gather.2.cloned.1.call-update) | async-done | bytes 14352400 | tf_op jit(solution)/shard_map/all_gather | solution.py:143
  130.0 4.0 fusion.17.q_ref.k_ref.v_ref
  134.0 9.4 %attn_fwd.1 = (bf16[512,768]{1,0:T(8,128)(2,1)S(1)}, f32[512,768]{1,0:T(8,128)S(1)}) custom-call(bf16[512,2304]{1,0:T(8,128)(2,1)S(1)} %fusion.17.q_ref.k_ref.v_ref, bf16[512,2304]{1,0:T(8,128)(2,1)S(1)} %fusion.17.q_ref.k_ref.v_ref, bf16[512,2304]{1,0:T(8,128)(2,1)S(1)} %fusion.17.q_ref.k_ref.v_ref, s32[512,1]{1,0:T(8,128)S(1)} %copy.118.segc_ref, ...), custom_call_target="tpu_custom_call" | custom-call | tf_op jit(solution)/shard_map/attn_fwd/pallas_call | solution.py:85
  150.0 2.6 fusion.250
  153.4 4.0 slice.347
  157.4 6.7 %slice.282 = bf16[2304,768]{1,0:T(8,128)(2,1)} reshape(bf16[576,3072]{1,0:T(8,128)(2,1)} %slice.347) | data formatting | bytes 7077888 | tf_op jit(solution)/shard_map/slice | solution.py:174
  166.4 3.3 fusion.185
  169.8 5.7 multiply_convert_fusion.2
  182.6 2.4 slice.336
  185.0 3.1 slice.267
  188.1 3.6 multiply_convert_fusion.5
  194.4 3.2 slice.343
  197.6 5.3 slice.276
  202.9 5.3 multiply_convert_fusion.3
  213.4 4.9 slice.351
  218.3 8.5 %reshape.387 = bf16[3072,768]{1,0:T(8,128)(2,1)} reshape(bf16[768,3072]{1,0:T(8,128)(2,1)} %slice.351) | data formatting | bytes 9437184 | tf_op jit(solution)/shard_map/reshape | solution.py:147
  226.8 5.5 multiply_convert_fusion.1
  234.6 2.8 fusion.251
  238.9 2.4 fusion.120
  241.4 3.9 convert_reduce_fusion.4
  247.2 4.6 multiply_convert_fusion
  260.1 2.4 convert_reduce_fusion.7
  262.6 3.3 fusion.12
  269.7 4.6 fusion.174
  274.3 4.1 fusion.179
  278.5 2.4 convolution_add_fusion.3
  281.7 9.3 %multiply_reduce_fusion = (f32[768]{0:T(1024)}, f32[512]{0:T(512)S(1)}, f32[512]{0:T(512)S(1)}, f32[768]{0:T(1024)}, f32[768]{0:T(1024)}, /*index=5*/f32[512]{0:...) fusion(f32[512,768]{1,0:T(8,128)S(1)} %copy-done.12, ...), kind=kOutput, calls=%fused_computation.179 | convolution fusion | flops 2433603584 | bytes 22878208 | tf_op jit(solution)/shard_map/dot_general | solution.py:31
  291.0 4.9 fusion.235
  312.9 2.6 convolution_convert_fusion.8
  321.9 15.3 %attn_bwd.1 = (bf16[512,768]{1,0:T(8,128)(2,1)S(1)}, bf16[512,768]{1,0:T(8,128)(2,1)S(1)}, bf16[512,768]{1,0:T(8,128)(2,1)S(1)}) custom-call(bf16[512,2304]{1,0:T(8,128)(2,1)} %copy-done, bf16[512,2304]{1,0:T(8,128)(2,1)} %copy-done, bf16[512,2304]{1,0:T(8,128)(2,1)} %copy-done, bf16[512,768]{1,0:T(8,128)(2,1)S(1)} %pad_maximum_fusion.1.g_ref, ...), custom_call_target="tpu_custom_call" | custom-call | tf_op jit(solution)/shard_map/attn_bwd/pallas_call | solution.py:102
  340.1 3.2 fusion.144
  343.5 2.8 fusion.164
  348.5 2.5 pad_maximum_fusion
  350.9 8.6 %convert_element_type.229 = bf16[768,3072]{1,0:T(8,128)(2,1)} reshape(bf16[3072,768]{1,0:T(8,128)(2,1)} %pad_maximum_fusion) | data formatting | bytes 9437184 | tf_op jit(solution)/shard_map/convert_element_type | solution.py:244
  359.6 3.6 fusion.149
  364.8 5.1 fusion.159
  370.0 2.6 copy.131
  372.6 6.2 %fusion.169 = bf16[768,768]{0,1:T(8,128)(2,1)} fusion(bf16[512,768]{1,0:T(8,128)(2,1)} %get-tuple-element.185, bf16[512,768]{1,0:T(8,128)(2,1)S(1)} %copy-done.50, bf16[512,768]{1,0:T(8,128)(2,1)} %get-tuple-element.200, bf16[512,768]{1,0:T(8,128)(2,1)} %copy-done.115, bf16[512,768]{1,0:T(8,128)(2,1)} %get-tuple-element.220, ...), kind=kOutput, calls=%fused_computation.222 | convolution fusion | flops 2441674752 | bytes 7471104 | tf_op jit(solution)/shard_map/dot_general | solution.py:27
  378.8 2.4 copy.130
  381.3 5.5 fusion.11
  386.7 5.8 copy.129
  392.5 4.1 constant_dynamic-update-slice_fusion.15
  396.6 2.4 copy.133
  401.4 2.4 constant_dynamic-update-slice_fusion.14
  403.8 2.4 constant_dynamic-update-slice_fusion.13
  409.0 2.5 constant_dynamic-update-slice_fusion.10
  417.3 5.6 add_bitcast_fusion
  422.9 148.9 %reduce-scatter.4.cloned.1.call-done = bf16[24,9344]{1,0:T(8,128)(2,1)} async-done(((bf16[768,9344]{1,0:T(8,128)(2,1)}), bf16[24,9344]{1,0:T(8,128)(2,1)}) %reduce-scatter.4.cloned.1.call-update) | async-done | bytes 448528
  (391 shorter events, 108.1 us)
Async XLA Ops:
  7.2 12.8 %copy-start.3 = (s32[1,512]{1,0:T(1,128)S(1)}, s32[1,512]{1,0:T(1,128)}, u32[]{:S(2)}) copy-start(s32[1,512]{1,0:T(1,128)} %segr_ref.3) | copy-start | bytes 6148
  7.2 118.9 %all-gather.2.cloned.1.call-start = ((), (), s32[]{:S(2)}) async-start(), calls=%async_computation.1 | async-start | bytes 14800896 | tf_op jit(solution)/shard_map/all_gather | solution.py:143
  19.9 551.9 %reduce-scatter.4.cloned.1.call-start = ((), (), s32[]{:S(2)}) async-start(), calls=%async_computation.2 | async-start | bytes 14800896
  130.0 61.8 %copy-start.99 = (f32[768]{0:T(1024)}, f32[768]{0:T(1024)S(1)}, u32[]{:S(2)}) copy-start(f32[768]{0:T(1024)S(1)} %get-tuple-element.151) | copy-start | bytes 9220
  134.0 9.4 %copy-start = (bf16[512,2304]{1,0:T(8,128)(2,1)}, bf16[512,2304]{1,0:T(8,128)(2,1)S(1)}, u32[]{:S(2)}) copy-start(bf16[512,2304]{1,0:T(8,128)(2,1)S(1)} %fusion.17.q_ref.k_ref.v_ref) | copy-start | bytes 7077892
  148.4 61.1 %copy-start.76 = (f32[512]{0:T(512)}, f32[512]{0:T(512)S(1)}, u32[]{:S(2)}) copy-start(f32[512]{0:T(512)S(1)} %broadcast_multiply_fusion.21) | copy-start | bytes 6148
  150.0 26.9 %copy-start.80 = (f32[512]{0:T(512)}, f32[512]{0:T(512)S(1)}, u32[]{:S(2)}) copy-start(f32[512]{0:T(512)S(1)} %add_rsqrt_fusion.3) | copy-start | bytes 6148
  150.0 59.5 %copy-start.90 = (f32[512]{0:T(512)}, f32[512]{0:T(512)S(1)}, u32[]{:S(2)}) copy-start(f32[512]{0:T(512)S(1)} %add_rsqrt_fusion.5) | copy-start | bytes 6148
  150.0 41.8 %copy-start.73 = (f32[512]{0:T(512)}, f32[512]{0:T(512)S(1)}, u32[]{:S(2)}) copy-start(f32[512]{0:T(512)S(1)} %broadcast_multiply_fusion.23) | copy-start | bytes 6148
  152.6 81.3 %copy-start.78 = (f32[512]{0:T(512)}, f32[512]{0:T(512)S(1)}, u32[]{:S(2)}) copy-start(f32[512]{0:T(512)S(1)} %broadcast_multiply_fusion.17) | copy-start | bytes 6148
  166.2 25.5 %copy-start.88 = (f32[512]{0:T(512)}, f32[512]{0:T(512)S(1)}, u32[]{:S(2)}) copy-start(f32[512]{0:T(512)S(1)} %get-tuple-element.258) | copy-start | bytes 6148
  166.3 67.6 %copy-start.92 = (f32[512]{0:T(512)}, f32[512]{0:T(512)S(1)}, u32[]{:S(2)}) copy-start(f32[512]{0:T(512)S(1)} %get-tuple-element.257) | copy-start | bytes 6148
  166.4 3.3 copy-start.103
  169.7 5.7 copy-start.57
  180.5 4.5 copy-start.82
  188.1 3.7 copy-start.42
  192.8 45.0 %copy-start.84 = (f32[512]{0:T(512)}, f32[512]{0:T(512)S(1)}, u32[]{:S(2)}) copy-start(f32[512]{0:T(512)S(1)} %broadcast_multiply_fusion.22) | copy-start | bytes 6148
  194.2 43.6 %copy-start.95 = (f32[512]{0:T(512)}, f32[512]{0:T(512)S(1)}, u32[]{:S(2)}) copy-start(f32[512]{0:T(512)S(1)} %add_rsqrt_fusion.6) | copy-start | bytes 6148
  202.9 6.6 %copy-start.35 = (bf16[1536,768]{1,0:T(8,128)(2,1)S(1)}, bf16[1536,768]{1,0:T(8,128)(2,1)}, u32[]{:S(2)}) copy-start(bf16[1536,768]{1,0:T(8,128)(2,1)} %slice.276) | copy-start | bytes 7077892
  211.7 26.1 %copy-start.86 = (f32[512]{0:T(512)}, f32[512]{0:T(512)S(1)}, u32[]{:S(2)}) copy-start(f32[512]{0:T(512)S(1)} %broadcast_multiply_fusion.20) | copy-start | bytes 6148
  213.2 24.7 %copy-start.97 = (f32[512]{0:T(512)}, f32[512]{0:T(512)S(1)}, u32[]{:S(2)}) copy-start(f32[512]{0:T(512)S(1)} %add_rsqrt_fusion.4) | copy-start | bytes 6148
  213.4 13.4 %copy-start.101 = (f32[3072]{0:T(1024)}, f32[3072]{0:T(1024)S(1)}, u32[]{:S(2)}) copy-start(f32[3072]{0:T(1024)S(1)} %add.564) | copy-start | bytes 36868
  218.3 8.6 %copy-start.59 = (bf16[512,768]{1,0:T(8,128)(2,1)S(1)}, bf16[512,768]{1,0:T(8,128)(2,1)}, u32[]{:S(2)}) copy-start(bf16[512,768]{1,0:T(8,128)(2,1)} %get-tuple-element.220) | copy-start | bytes 2359300
  226.8 7.0 %copy-start.22 = (bf16[3072,768]{1,0:T(8,128)(2,1)S(1)}, bf16[3072,768]{1,0:T(8,128)(2,1)}, u32[]{:S(2)}) copy-start(bf16[3072,768]{1,0:T(8,128)(2,1)} %reshape.387) | copy-start | bytes 14155780
  245.3 9.3 %copy-start.63 = (bf16[512,768]{1,0:T(8,128)(2,1)}, bf16[512,768]{1,0:T(8,128)(2,1)S(1)}, u32[]{:S(2)}) copy-start(bf16[512,768]{1,0:T(8,128)(2,1)S(1)} %get-tuple-element.180) | copy-start | bytes 2359300
  251.8 3.4 copy-start.36
  251.8 4.6 copy-start.114
  251.9 10.7 %slice-start.2 = ((s8[4718592]{0:T(1024)(128)(4,1)}), s8[524288]{0:T(1024)(128)(4,1)S(1)}, s32[]{:S(2)}) async-start(s8[4718592]{0:T(1024)(128)(4,1)} %bitcast.184), calls=%async_computation.5 | async-start | bytes 1048576
  256.4 6.2 %slice-start.3 = ((s8[4718592]{0:T(1024)(128)(4,1)}), s8[4194304]{0:T(1024)(128)(4,1)S(1)}, s32[]{:S(2)}) async-start(s8[4718592]{0:T(1024)(128)(4,1)} %bitcast.184), calls=%async_computation.6 | async-start | bytes 8388608
  262.6 3.3 copy-start.65
  262.6 4.9 copy-start.67
  269.7 8.7 %copy-start.115 = (bf16[512,768]{1,0:T(8,128)(2,1)}, bf16[512,768]{1,0:T(8,128)(2,1)S(1)}, u32[]{:S(2)}) copy-start(bf16[512,768]{1,0:T(8,128)(2,1)S(1)} %get-tuple-element.254) | copy-start | bytes 2359300
  295.9 4.4 copy-start.13
  301.5 3.7 copy-start.107
  301.5 3.7 copy-start.108
  301.5 3.7 copy-start.109
  301.6 3.7 copy-start.110
  301.6 3.8 copy-start.34
  312.8 3.9 copy-start.14
  315.5 5.1 copy-start.44
  340.0 3.3 copy-start.62
  340.1 3.5 copy-start.113
  350.9 8.6 %copy-start.52 = (bf16[512,768]{1,0:T(8,128)(2,1)S(1)}, bf16[512,768]{1,0:T(8,128)(2,1)}, u32[]{:S(2)}) copy-start(bf16[512,768]{1,0:T(8,128)(2,1)} %get-tuple-element.189) | copy-start | bytes 2359300
  350.9 8.6 %copy-start.56 = (bf16[512,768]{1,0:T(8,128)(2,1)S(1)}, bf16[512,768]{1,0:T(8,128)(2,1)}, u32[]{:S(2)}) copy-start(bf16[512,768]{1,0:T(8,128)(2,1)} %get-tuple-element.183) | copy-start | bytes 2359300
  350.9 8.6 %copy-start.58 = (bf16[512,768]{1,0:T(8,128)(2,1)S(1)}, bf16[512,768]{1,0:T(8,128)(2,1)}, u32[]{:S(2)}) copy-start(bf16[512,768]{1,0:T(8,128)(2,1)} %copy-done.57) | copy-start | bytes 2359300
  392.5 16.5 %slice-start = ((s8[4718592]{0:T(1024)(128)(4,1)}), s8[524288]{0:T(1024)(128)(4,1)S(1)}, s32[]{:S(2)}) async-start(s8[4718592]{0:T(1024)(128)(4,1)} %bitcast.174), calls=%async_computation.3 | async-start | bytes 1048576
  399.1 9.9 %slice-start.1 = ((s8[4718592]{0:T(1024)(128)(4,1)}), s8[4194304]{0:T(1024)(128)(4,1)S(1)}, s32[]{:S(2)}) async-start(s8[4718592]{0:T(1024)(128)(4,1)} %bitcast.174), calls=%async_computation.4 | async-start | bytes 8388608
  413.9 3.4 copy-start.72
  (74 other events, 168.3 us)
Sparse Core Ops, SparseCore 0:
  20.1 105.9 all-gather.1
  412.4 159.3 reduce-scatter.3
